TPU v7x, 32 devices: a whole 2x2x4 slice. The times are simulated.
32 devices in a mesh: gx: 2 (over y), gy: 4 (over z), gz: 4 (over x, core).
Axes of the slice: x: 2, y: 2, z: 4, core: 2. Of those that a mesh axis runs over, the one named last changes fastest.
Arguments:
- velocity: float32 [8192, 3, 128], P(('gx', 'gy', 'gz')), may hold values from -6 to 6
- cell_index: int32 [8192, 128], P(('gx', 'gy', 'gz')), may hold values from 0 to 5804
- block_target: int32 [8192, 1], P(('gx', 'gy', 'gz')), may hold values from 0 to 31; in each aligned block of 256 rows (0 to 255, 256 to 511, ...) at most 12 rows name the same one
- rotation_axis: int32 [32, 32, 32], replicated, may hold values from 0 to 63
- grid_shift: int32 [3], replicated, may hold values from 0 to 31
Outputs:
- brick_velocity: float32 [32, 32, 12, 3, 128], P(('gx', 'gy', 'gz'))
- cell_flow: float32 [3, 8, 32, 512], P(None, 'gx', 'gy', 'gz')
Inputs may be any that keep to these rules, and one draw needn't show every extreme that they name: `block_target`: among the blocks that one device holds, no brick is named by more than 12 blocks, a bound that some block reaches.
All inputs are finite; a program needn't handle non-finite values.
Results may differ from a plain program's by a relative error of at most 0.0003.
Values sent between devices are 32-bit elements; how exact they have to be, the bound alone decides.
A program may use at most 64 MiB of HBM per device.

v0:
```python
import jax
import jax.numpy as jnp
from jax import lax
from jax.sharding import PartitionSpec as P

CX = 4
CY = 8
CZ = 128
NAX = 64
APER = 32


angle_cosine = -0.6427876096865393
angle_sine = 0.766044443118978
highest = lax.Precision.HIGHEST


def with_halo(cells, sides, width):
    for axis, dim in sides:
        count = lax.axis_size(axis)
        head = lax.slice_in_dim(cells, 0, width, axis=dim)
        tail = lax.slice_in_dim(cells, cells.shape[dim] - width, cells.shape[dim], axis=dim)
        cells = jnp.concatenate(
            [
                lax.ppermute(tail, axis, [(i, (i + 1) % count) for i in range(count)]),
                cells,
                lax.ppermute(head, axis, [((i + 1) % count, i) for i in range(count)]),
            ],
            axis=dim,
        )
    return cells


def axis_table():
    counter = jnp.arange(NAX, dtype=jnp.float32) + 0.5
    height = 1.0 - 2.0 * counter / NAX
    radius = jnp.sqrt(jnp.maximum(1.0 - height * height, 0.0))
    turning = counter * 2.399963229728653
    return jnp.stack([radius * jnp.cos(turning), radius * jnp.sin(turning), height])


def rotate_about(direction, relative):
    inner_product = (
        direction[0] * relative[0] + direction[1] * relative[1] + direction[2] * relative[2]
    )
    crossed = [
        direction[1] * relative[2] - direction[2] * relative[1],
        direction[2] * relative[0] - direction[0] * relative[2],
        direction[0] * relative[1] - direction[1] * relative[0],
    ]
    return [
        relative[component] * angle_cosine
        + crossed[component] * angle_sine
        + direction[component] * inner_product * (1.0 - angle_cosine)
        for component in range(3)
    ]


def fold_rims(padded, dimension, length):
    inside = lax.slice_in_dim(padded, 1, length + 1, axis=dimension)
    lowest = lax.slice_in_dim(padded, 0, 1, axis=dimension)
    highest_rim = lax.slice_in_dim(padded, length + 1, length + 2, axis=dimension)
    position = lax.broadcasted_iota(jnp.int32, inside.shape, dimension)
    return (
        inside
        + jnp.where(position == 0, lowest, 0.0)
        + jnp.where(position == length - 1, highest_rim, 0.0)
    )


def plane_onehot(labels, planes):
    plane = jnp.where(labels >= 0, labels // (CZ + 1), -1)
    return (jnp.arange(planes, dtype=jnp.int32)[:, None] == plane[None, :]).astype(jnp.float32)


def depth_onehot(labels):
    depth = jnp.where(labels >= 0, labels % (CZ + 1), -1)
    return (depth[:, None] == jnp.arange(CZ + 1, dtype=jnp.int32)[None, :]).astype(jnp.float32)


def lookup_table(rotation_axis, index_x, index_y, index_z):
    table = rotation_axis.astype(jnp.float32)
    pick_x = (index_x[:, None] == jnp.arange(APER, dtype=jnp.int32)[None, :]).astype(jnp.float32)
    pick_y = (index_y[:, None] == jnp.arange(APER, dtype=jnp.int32)[None, :]).astype(jnp.float32)
    pick_z = (index_z[:, None] == jnp.arange(APER, dtype=jnp.int32)[None, :]).astype(jnp.float32)
    section = jnp.einsum("xa,abc->xbc", pick_x, table, precision=highest)
    section = jnp.einsum("xbc,yb->xyc", section, pick_y, precision=highest)
    section = jnp.einsum("xyc,zc->xyz", section, pick_z, precision=highest)
    return (section + 0.5).astype(jnp.int32)


def shards(velocity, cell_index, block_target, rotation_axis, grid_shift):
    devices = lax.axis_size(("gx", "gy", "gz"))
    blocks = velocity.shape[0]
    block_rows = velocity.shape[2]
    capacity = 3 * blocks // (2 * devices)
    slots = devices * capacity
    target = block_target[:, 0]
    target_onehot = (target[:, None] == jnp.arange(devices, dtype=jnp.int32)[None, :]).astype(
        jnp.float32
    )
    row_iota = lax.broadcasted_iota(jnp.int32, (blocks, blocks), 0)
    col_iota = lax.broadcasted_iota(jnp.int32, (blocks, blocks), 1)
    earlier = (row_iota > col_iota).astype(jnp.float32)
    before = jnp.dot(earlier, target_onehot, precision=highest)
    ranking = (jnp.sum(before * target_onehot, axis=1) + 0.5).astype(jnp.int32)
    places = target * capacity + ranking
    placing = (jnp.arange(slots, dtype=jnp.int32)[:, None] == places[None, :]).astype(jnp.float32)
    outgoing = jnp.dot(placing, velocity.reshape(blocks, 3 * block_rows), precision=highest)
    outgoing = outgoing.reshape(devices, capacity, 3, block_rows)
    shifted = jnp.dot(placing, (cell_index + 1).astype(jnp.float32), precision=highest)
    labels = (shifted + 0.5).astype(jnp.int32) - 1
    labels = labels.reshape(devices, capacity, block_rows)
    arriving = lax.all_to_all(outgoing, ("gx", "gy", "gz"), split_axis=0, concat_axis=0, tiled=True)
    received = lax.all_to_all(labels, ("gx", "gy", "gz"), split_axis=0, concat_axis=0, tiled=True)
    planes = (CX + 1) * (CY + 1)
    extended = planes * (CZ + 1)
    groups = 8
    group_labels = received.reshape(groups, -1)
    group_moving = jnp.transpose(
        arriving.reshape(groups, devices // groups, capacity, 3, block_rows), (0, 3, 1, 2, 4)
    ).reshape(groups, 3, -1)

    def add_group(totals, inputs):
        labels_here, moving_here = inputs
        filled_here = (labels_here >= 0).astype(jnp.float32)
        channels = jnp.concatenate([filled_here[None], moving_here], axis=0)
        weighted = (channels[:, None, :] * plane_onehot(labels_here, planes)[None]).reshape(
            4 * planes, -1
        )
        return (totals + jnp.dot(weighted, depth_onehot(labels_here), precision=highest), None)

    totals, unused = lax.scan(
        add_group, jnp.zeros((4 * planes, CZ + 1), jnp.float32), (group_labels, group_moving)
    )
    partial_value = totals.reshape(4, CX + 1, CY + 1, CZ + 1)
    folded = fold_rims(with_halo(partial_value, (("gx", 1),), 1), 1, CX + 1)
    folded = fold_rims(with_halo(folded, (("gy", 2),), 1), 2, CY + 1)
    folded = fold_rims(with_halo(folded, (("gz", 3),), 1), 3, CZ + 1)
    cell_means = folded[1:] / jnp.maximum(folded[0], 1.0)
    cell_flow = cell_means[:, :CX, :CY, :CZ]
    index_x = (
        (lax.axis_index("gx") * CX + jnp.arange(CX + 1, dtype=jnp.int32))
        % (CX * lax.axis_size("gx"))
        + grid_shift[0]
    ) % APER
    index_y = (
        (lax.axis_index("gy") * CY + jnp.arange(CY + 1, dtype=jnp.int32))
        % (CY * lax.axis_size("gy"))
        + grid_shift[1]
    ) % APER
    index_z = (
        (lax.axis_index("gz") * CZ + jnp.arange(CZ + 1, dtype=jnp.int32))
        % (CZ * lax.axis_size("gz"))
        + grid_shift[2]
    ) % APER
    picked = lookup_table(rotation_axis, index_x, index_y, index_z).reshape(-1)
    choose = (jnp.arange(NAX, dtype=jnp.int32)[:, None] == picked[None, :]).astype(jnp.float32)
    direction = jnp.dot(axis_table(), choose, precision=highest)
    cell_rows = jnp.concatenate([cell_means.reshape(3, extended), direction], axis=0)
    cell_rows = cell_rows.reshape(6 * planes, CZ + 1)

    def read_group(carry, labels_here):
        by_depth = jnp.dot(cell_rows, depth_onehot(labels_here).T, precision=highest)
        by_depth = by_depth.reshape(6, planes, -1)
        return (carry, jnp.sum(by_depth * plane_onehot(labels_here, planes)[None], axis=1))

    unused, picked_rows = lax.scan(read_group, jnp.zeros((), jnp.float32), group_labels)
    gathered = jnp.transpose(picked_rows, (1, 0, 2)).reshape(6, devices, capacity, block_rows)
    filled = received >= 0
    relative = [arriving[:, :, component, :] - gathered[component] for component in range(3)]
    turned = rotate_about([gathered[3], gathered[4], gathered[5]], relative)
    updated = jnp.stack(
        [jnp.where(filled, gathered[component] + turned[component], 0.0) for component in range(3)],
        axis=2,
    )
    return (updated[None], cell_flow)


def solution(mesh):
    return jax.shard_map(
        shards,
        mesh=mesh,
        in_specs=(
            P(("gx", "gy", "gz"), None, None),
            P(("gx", "gy", "gz"), None),
            P(("gx", "gy", "gz"), None),
            P(),
            P(),
        ),
        out_specs=(P(("gx", "gy", "gz"), None, None, None, None), P(None, "gx", "gy", "gz")),
        check_vma=False,
    )
```

profile of v0, /device:TPU:1, one launch (start us, length us, event | category | flops | bytes accessed | tf_op | source)
XLA Modules:
  0.0 316.4 jit_solution(10936807395658888919)
XLA Ops:
  4.3 7.1 %all-to-all-start = ((s32[32,12,128]{2,1,0:T(8,128)}), s32[32,12,128]{2,1,0:T(8,128)S(1)}, u32[]{:S(2)}, u32[]{:S(2)}) async-start(s32[32,12,128]{2,1,0:T(8,128)} %reshape.312), calls=%async_computation | async-start | bytes 524288 | tf_op jit(solution)/shard_map/all_to_all | solution.py:115
  15.3 6.4 %all-to-all-done = s32[32,12,128]{2,1,0:T(8,128)S(1)} async-done(((s32[32,12,128]{2,1,0:T(8,128)}), s32[32,12,128]{2,1,0:T(8,128)S(1)}, u32[]{:S(2)}, u32[]{:S(2)}) %all-to-all-start) | async-done | bytes 196640 | tf_op jit(solution)/shard_map/all_to_all | solution.py:115
  26.6 18.4 %all-to-all-done.1 = f32[32,12,3,128]{3,2,1,0:T(4,128)S(1)} async-done(((f32[32,12,3,128]{3,2,1,0:T(4,128)}), f32[32,12,3,128]{3,2,1,0:T(4,128)S(1)}, u32[]{:S(2)}, u32[]{:S(2)}) %all-to-all-start.1) | async-done | bytes 589856 | tf_op jit(solution)/shard_map/all_to_all | solution.py:114
  45.3 107.4 %while.26 = (s32[]{:T(128)}, f32[180,129]{0,1:T(8,128)S(1)}, s32[8,6144]{1,0:T(8,128)S(1)}, f32[8,3,6144]{2,0,1:T(8,128)S(1)}, s32[]{:T(128)}, /*index=5*/s32[]{:T(128)}) while((s32[]{:T(128)}, f32[180,129]{0,1:T(8,128)S(1)}, s32[8,6144]{1,0:T(8,128)S(1)}, f32[8,3,6144]{2,0,1:T(8,128)S(1)}, s32[]{:T(128)}, ...), condition=%wide.region_2.3_spmd.clone, body=%wide.region_1.2_spmd.clone.sunk | while | flops 1714597248 | bytes 20915708 | solution.py:133
  48.5 5.0 %mul.283 = f32[180,6144]{1,0:T(8,128)} reshape(f32[4,45,6144]{2,1,0:T(8,128)} %broadcast_multiply_fusion.2) | data formatting | bytes 8847360 | tf_op jit(solution)/shard_map/while/body/eval_jaxpr/mul | solution.py:128
  53.5 5.2 %fusion.84 = f32[180,129]{0,1:T(8,128)S(1)} fusion(f32[180,6144]{1,0:T(8,128)} %mul.283, s32[6144]{0:T(1024)S(1)} %fusion.83, f32[180,129]{0,1:T(8,128)S(1)} %get-tuple-element.278, pred[]{:T(512)S(6)} %compare.27), kind=kOutput, calls=%fused_computation.19.clone.1 | convolution fusion | flops 1712803200 | bytes 4634017 | tf_op jit(solution)/shard_map/while/body/eval_jaxpr/dot_general | solution.py:131
  61.9 5.0 %mul.283 = f32[180,6144]{1,0:T(8,128)} reshape(f32[4,45,6144]{2,1,0:T(8,128)} %broadcast_multiply_fusion.2) | data formatting | bytes 8847360 | tf_op jit(solution)/shard_map/while/body/eval_jaxpr/mul | solution.py:128
  66.9 5.2 %fusion.84 = f32[180,129]{0,1:T(8,128)S(1)} fusion(f32[180,6144]{1,0:T(8,128)} %mul.283, s32[6144]{0:T(1024)S(1)} %fusion.83, f32[180,129]{0,1:T(8,128)S(1)} %get-tuple-element.278, pred[]{:T(512)S(6)} %compare.27), kind=kOutput, calls=%fused_computation.19.clone.1 | convolution fusion | flops 1712803200 | bytes 4634017 | tf_op jit(solution)/shard_map/while/body/eval_jaxpr/dot_general | solution.py:131
  75.3 5.0 %mul.283 = f32[180,6144]{1,0:T(8,128)} reshape(f32[4,45,6144]{2,1,0:T(8,128)} %broadcast_multiply_fusion.2) | data formatting | bytes 8847360 | tf_op jit(solution)/shard_map/while/body/eval_jaxpr/mul | solution.py:128
  80.3 5.2 %fusion.84 = f32[180,129]{0,1:T(8,128)S(1)} fusion(f32[180,6144]{1,0:T(8,128)} %mul.283, s32[6144]{0:T(1024)S(1)} %fusion.83, f32[180,129]{0,1:T(8,128)S(1)} %get-tuple-element.278, pred[]{:T(512)S(6)} %compare.27), kind=kOutput, calls=%fused_computation.19.clone.1 | convolution fusion | flops 1712803200 | bytes 4634017 | tf_op jit(solution)/shard_map/while/body/eval_jaxpr/dot_general | solution.py:131
  88.7 5.0 %mul.283 = f32[180,6144]{1,0:T(8,128)} reshape(f32[4,45,6144]{2,1,0:T(8,128)} %broadcast_multiply_fusion.2) | data formatting | bytes 8847360 | tf_op jit(solution)/shard_map/while/body/eval_jaxpr/mul | solution.py:128
  93.7 5.2 %fusion.84 = f32[180,129]{0,1:T(8,128)S(1)} fusion(f32[180,6144]{1,0:T(8,128)} %mul.283, s32[6144]{0:T(1024)S(1)} %fusion.83, f32[180,129]{0,1:T(8,128)S(1)} %get-tuple-element.278, pred[]{:T(512)S(6)} %compare.27), kind=kOutput, calls=%fused_computation.19.clone.1 | convolution fusion | flops 1712803200 | bytes 4634017 | tf_op jit(solution)/shard_map/while/body/eval_jaxpr/dot_general | solution.py:131
  102.2 5.0 %mul.283 = f32[180,6144]{1,0:T(8,128)} reshape(f32[4,45,6144]{2,1,0:T(8,128)} %broadcast_multiply_fusion.2) | data formatting | bytes 8847360 | tf_op jit(solution)/shard_map/while/body/eval_jaxpr/mul | solution.py:128
  107.2 5.2 %fusion.84 = f32[180,129]{0,1:T(8,128)S(1)} fusion(f32[180,6144]{1,0:T(8,128)} %mul.283, s32[6144]{0:T(1024)S(1)} %fusion.83, f32[180,129]{0,1:T(8,128)S(1)} %get-tuple-element.278, pred[]{:T(512)S(6)} %compare.27), kind=kOutput, calls=%fused_computation.19.clone.1 | convolution fusion | flops 1712803200 | bytes 4634017 | tf_op jit(solution)/shard_map/while/body/eval_jaxpr/dot_general | solution.py:131
  115.6 5.0 %mul.283 = f32[180,6144]{1,0:T(8,128)} reshape(f32[4,45,6144]{2,1,0:T(8,128)} %broadcast_multiply_fusion.2) | data formatting | bytes 8847360 | tf_op jit(solution)/shard_map/while/body/eval_jaxpr/mul | solution.py:128
  120.6 5.2 %fusion.84 = f32[180,129]{0,1:T(8,128)S(1)} fusion(f32[180,6144]{1,0:T(8,128)} %mul.283, s32[6144]{0:T(1024)S(1)} %fusion.83, f32[180,129]{0,1:T(8,128)S(1)} %get-tuple-element.278, pred[]{:T(512)S(6)} %compare.27), kind=kOutput, calls=%fused_computation.19.clone.1 | convolution fusion | flops 1712803200 | bytes 4634017 | tf_op jit(solution)/shard_map/while/body/eval_jaxpr/dot_general | solution.py:131
  129.0 5.0 %mul.283 = f32[180,6144]{1,0:T(8,128)} reshape(f32[4,45,6144]{2,1,0:T(8,128)} %broadcast_multiply_fusion.2) | data formatting | bytes 8847360 | tf_op jit(solution)/shard_map/while/body/eval_jaxpr/mul | solution.py:128
  134.0 5.2 %fusion.84 = f32[180,129]{0,1:T(8,128)S(1)} fusion(f32[180,6144]{1,0:T(8,128)} %mul.283, s32[6144]{0:T(1024)S(1)} %fusion.83, f32[180,129]{0,1:T(8,128)S(1)} %get-tuple-element.278, pred[]{:T(512)S(6)} %compare.27), kind=kOutput, calls=%fused_computation.19.clone.1 | convolution fusion | flops 1712803200 | bytes 4634017 | tf_op jit(solution)/shard_map/while/body/eval_jaxpr/dot_general | solution.py:131
  142.5 5.0 %mul.283 = f32[180,6144]{1,0:T(8,128)} reshape(f32[4,45,6144]{2,1,0:T(8,128)} %broadcast_multiply_fusion.2) | data formatting | bytes 8847360 | tf_op jit(solution)/shard_map/while/body/eval_jaxpr/mul | solution.py:128
  147.5 5.2 %fusion.84 = f32[180,129]{0,1:T(8,128)S(1)} fusion(f32[180,6144]{1,0:T(8,128)} %mul.283, s32[6144]{0:T(1024)S(1)} %fusion.83, f32[180,129]{0,1:T(8,128)S(1)} %get-tuple-element.278, pred[]{:T(512)S(6)} %compare.27), kind=kOutput, calls=%fused_computation.19.clone.1 | convolution fusion | flops 1712803200 | bytes 4634017 | tf_op jit(solution)/shard_map/while/body/eval_jaxpr/dot_general | solution.py:131
  172.6 133.5 %while.25 = (s32[]{:T(128)}, f32[8,6,6144]{2,1,0:T(8,128)}, s32[8,6144]{1,0:T(8,128)S(1)}, f32[270,129]{1,0:T(8,128)S(1)}, s32[]{:T(128)}) while((s32[]{:T(128)}, f32[8,6,6144]{2,1,0:T(8,128)}, s32[8,6144]{1,0:T(8,128)S(1)}, f32[270,129]{1,0:T(8,128)S(1)}, s32[]{:T(128)}) %tuple.97), condition=%wide.region_5.6_spmd, body=%wide.region_3.5_spmd.sunk | while | flops 2572677120 | bytes 29594236 | solution.py:168
  177.8 6.6 %reshape.334 = f32[6,45,6144]{2,1,0:T(8,128)} reshape(f32[270,6144]{1,0:T(8,128)} %convolution_bitcast_fusion.3) | data formatting | bytes 13271040 | tf_op jit(solution)/shard_map/while/body/eval_jaxpr/reshape | solution.py:165
  194.4 6.6 %reshape.334 = f32[6,45,6144]{2,1,0:T(8,128)} reshape(f32[270,6144]{1,0:T(8,128)} %convolution_bitcast_fusion.3) | data formatting | bytes 13271040 | tf_op jit(solution)/shard_map/while/body/eval_jaxpr/reshape | solution.py:165
  206.3 4.8 %convolution_bitcast_fusion.3 = f32[270,6144]{1,0:T(8,128)} fusion(f32[270,129]{1,0:T(8,128)S(1)} %get-tuple-element.302, s32[6144]{0:T(1024)S(1)} %fusion.78), kind=kOutput, calls=%fused_computation.clone.1 | convolution fusion | flops 2568738816 | bytes 6799416 | tf_op jit(solution)/shard_map/while/body/eval_jaxpr/dot_general | solution.py:164
  211.1 6.6 %reshape.334 = f32[6,45,6144]{2,1,0:T(8,128)} reshape(f32[270,6144]{1,0:T(8,128)} %convolution_bitcast_fusion.3) | data formatting | bytes 13271040 | tf_op jit(solution)/shard_map/while/body/eval_jaxpr/reshape | solution.py:165
  227.8 6.6 %reshape.334 = f32[6,45,6144]{2,1,0:T(8,128)} reshape(f32[270,6144]{1,0:T(8,128)} %convolution_bitcast_fusion.3) | data formatting | bytes 13271040 | tf_op jit(solution)/shard_map/while/body/eval_jaxpr/reshape | solution.py:165
  239.6 4.8 %convolution_bitcast_fusion.3 = f32[270,6144]{1,0:T(8,128)} fusion(f32[270,129]{1,0:T(8,128)S(1)} %get-tuple-element.302, s32[6144]{0:T(1024)S(1)} %fusion.78), kind=kOutput, calls=%fused_computation.clone.1 | convolution fusion | flops 2568738816 | bytes 6799416 | tf_op jit(solution)/shard_map/while/body/eval_jaxpr/dot_general | solution.py:164
  244.5 6.6 %reshape.334 = f32[6,45,6144]{2,1,0:T(8,128)} reshape(f32[270,6144]{1,0:T(8,128)} %convolution_bitcast_fusion.3) | data formatting | bytes 13271040 | tf_op jit(solution)/shard_map/while/body/eval_jaxpr/reshape | solution.py:165
  261.1 6.6 %reshape.334 = f32[6,45,6144]{2,1,0:T(8,128)} reshape(f32[270,6144]{1,0:T(8,128)} %convolution_bitcast_fusion.3) | data formatting | bytes 13271040 | tf_op jit(solution)/shard_map/while/body/eval_jaxpr/reshape | solution.py:165
  277.8 6.6 %reshape.334 = f32[6,45,6144]{2,1,0:T(8,128)} reshape(f32[270,6144]{1,0:T(8,128)} %convolution_bitcast_fusion.3) | data formatting | bytes 13271040 | tf_op jit(solution)/shard_map/while/body/eval_jaxpr/reshape | solution.py:165
  294.5 6.6 %reshape.334 = f32[6,45,6144]{2,1,0:T(8,128)} reshape(f32[270,6144]{1,0:T(8,128)} %convolution_bitcast_fusion.3) | data formatting | bytes 13271040 | tf_op jit(solution)/shard_map/while/body/eval_jaxpr/reshape | solution.py:165
  306.1 8.3 %slice_reduce_fusion.1 = (f32[8,6144]{1,0:T(8,128)S(1)}, f32[8,6144]{1,0:T(8,128)S(1)}, f32[8,6144]{1,0:T(8,128)S(1)}, f32[8,6144]{1,0:T(8,128)S(1)}, f32[8,6144]{1,0:T(8,128)S(1)}, /*index=5*/f32[8,6144]{1,0:T(8,128)S(1)}) fusion(f32[6,8,6144]{2,0,1:T(8,128)} %bitcast.27), kind=kLoop, calls=%fused_computation.68 | loop fusion | bytes 2359296 | tf_op jit(solution)/shard_map/slice | solution.py:171
  (198 shorter events, 130.1 us)
Async XLA Ops:
  0.6 10.7 %copy-start.1 = (f32[256,3,128]{2,0,1:T(8,128)S(1)}, f32[256,3,128]{2,0,1:T(8,128)}, u32[]{:S(2)}) copy-start(f32[256,3,128]{2,0,1:T(8,128)} %param.9) | copy-start | bytes 1179652
  1.6 10.5 %copy-start.2 = (s32[3]{0:T(128)S(1)}, s32[3]{0:T(128)}, u32[]{:S(2)}) copy-start(s32[3]{0:T(128)} %param.13) | copy-start | bytes 40
  4.3 17.4 %all-to-all-start = ((s32[32,12,128]{2,1,0:T(8,128)}), s32[32,12,128]{2,1,0:T(8,128)S(1)}, u32[]{:S(2)}, u32[]{:S(2)}) async-start(s32[32,12,128]{2,1,0:T(8,128)} %reshape.312), calls=%async_computation | async-start | bytes 524288 | tf_op jit(solution)/shard_map/all_to_all | solution.py:115
  11.4 2.6 copy-start
  21.7 23.4 %all-to-all-start.1 = ((f32[32,12,3,128]{3,2,1,0:T(4,128)}), f32[32,12,3,128]{3,2,1,0:T(4,128)S(1)}, u32[]{:S(2)}, u32[]{:S(2)}) async-start(f32[32,12,3,128]{3,2,1,0:T(4,128)} %copy.87), calls=%async_computation.1 | async-start | bytes 1572864 | tf_op jit(solution)/shard_map/all_to_all | solution.py:114
  152.9 3.2 %collective-permute-start = (f32[4,1,9,129]{3,2,1,0:T(8,128)S(1)}, f32[4,1,9,129]{3,2,1,0:T(8,128)S(1)}, u32[]{:S(2)}, u32[]{:S(2)}) collective-permute-start(f32[4,1,9,129]{3,2,1,0:T(8,128)S(1)} %get-tuple-element.196), channel_id=1, source_target_pairs={{0,16},{16,0},{1,17},{17,1},{2,18},{18,2},{3,19},{19,3},{4,20},{20... | collective-permute-start | bytes 55736 | tf_op jit(solution)/shard_map/ppermute | solution.py:25
  153.7 3.4 %collective-permute-start.1 = (f32[4,1,9,129]{3,2,1,0:T(8,128)S(1)}, f32[4,1,9,129]{3,2,1,0:T(8,128)S(1)}, u32[]{:S(2)}, u32[]{:S(2)}) collective-permute-start(f32[4,1,9,129]{3,2,1,0:T(8,128)S(1)} %get-tuple-element.197), channel_id=1, source_target_pairs={{16,0},{0,16},{17,1},{1,17},{18,2},{2,18},{19,3},{3,19},{20,4},{4,... | collective-permute-start | bytes 55736 | tf_op jit(solution)/shard_map/ppermute | solution.py:27
  157.3 4.5 %collective-permute-start.2 = (f32[4,5,1,129]{3,2,1,0:T(1,128)S(1)}, f32[4,5,1,129]{3,2,1,0:T(1,128)S(1)}, u32[]{:S(2)}, u32[]{:S(2)}) collective-permute-start(f32[4,5,1,129]{3,2,1,0:T(1,128)S(1)} %get-tuple-element.194), channel_id=1, source_target_pairs={{0,4},{4,8},{8,12},{12,0},{1,5},{5,9},{9,13},{13,1},{2,6},{6,10},{... | collective-permute-start | bytes 30968 | tf_op jit(solution)/shard_map/ppermute | solution.py:25
  157.9 3.9 %collective-permute-start.3 = (f32[4,5,1,129]{3,2,1,0:T(1,128)S(1)}, f32[4,5,1,129]{3,2,1,0:T(1,128)S(1)}, u32[]{:S(2)}, u32[]{:S(2)}) collective-permute-start(f32[4,5,1,129]{3,2,1,0:T(1,128)S(1)} %get-tuple-element.195), channel_id=1, source_target_pairs={{4,0},{8,4},{12,8},{0,12},{5,1},{9,5},{13,9},{1,13},{6,2},{10,6},{... | collective-permute-start | bytes 30968 | tf_op jit(solution)/shard_map/ppermute | solution.py:27
  162.1 7.0 %collective-permute-start.4 = (f32[4,5,9,1]{3,2,1,0:T(8,128)S(1)}, f32[4,5,9,1]{3,2,1,0:T(8,128)S(1)}, u32[]{:S(2)}, u32[]{:S(2)}) collective-permute-start(f32[4,5,9,1]{3,2,1,0:T(8,128)S(1)} %get-tuple-element.192), channel_id=1, source_target_pairs={{0,1},{1,2},{2,3},{3,0},{4,5},{5,6},{6,7},{7,4},{8,9},{9,10},{10,1... | collective-permute-start | bytes 2168 | tf_op jit(solution)/shard_map/ppermute | solution.py:25
  166.1 4.9 %collective-permute-start.5 = (f32[4,5,9,1]{3,2,1,0:T(8,128)S(1)}, f32[4,5,9,1]{3,2,1,0:T(8,128)S(1)}, u32[]{:S(2)}, u32[]{:S(2)}) collective-permute-start(f32[4,5,9,1]{3,2,1,0:T(8,128)S(1)} %get-tuple-element.193), channel_id=1, source_target_pairs={{1,0},{2,1},{3,2},{0,3},{5,4},{6,5},{7,6},{4,7},{9,8},{10,9},{11,1... | collective-permute-start | bytes 2168 | tf_op jit(solution)/shard_map/ppermute | solution.py:27
where the time goes:
time: 318 us; the launch traced here: 316 us
  local copies, waits for them, and re-layouts  114 us (36%)
  matrix products  84.8 us (27%)
  other arithmetic  64.3 us (20%)
  waiting for transfers between devices  33 us (10%)
  starting transfers between devices  18.4 us (6%)
    reshape x8, local copies, waits for them, and re-layouts, read_group(): by_depth = by_depth.reshape(6, planes, -1)  53 us
    dot_general x8, matrix products, add_group(): jnp.dot(weighted, depth_onehot(labels_here), precision=highest)  41.7 us
    mul x8, local copies, waits for them, and re-layouts, add_group(): channels[:, None, :] * plane_onehot(labels_here, planes)[None]  39.9 us
    dot_general x8, matrix products, read_group(): jnp.dot(cell_rows, depth_onehot(labels_here).T, precision=highest)  38.8 us
    reduce_sum x8, other arithmetic, read_group(): jnp.sum(by_depth * plane_onehot(labels_here, planes)[None], axis=1)  33.2 us
    mul x8, other arithmetic, add_group(): channels[:, None, :] * plane_onehot(labels_here, planes)[None]  21.2 us
    all_to_all x1, waiting for transfers between devices, shards(): lax.all_to_all(outgoing, ('gx', 'gy', 'gz'), split_axis=0, concat_axis=0,...  18.4 us
    slice x1, local copies, waits for them, and re-layouts, shards(): gathered[component]  8.34 us
  transfers between devices with their start and end apart: 8, of which 7 were waited for; matrix products, arithmetic and copies ran while one was open for 2% of the time, Pallas kernels for 0%

commit v1 on v0

v1 whole, which is shorter than its diff:
```python
import functools
import jax
import jax.numpy as jnp
from jax import lax
from jax.experimental import pallas as pl
from jax.experimental.pallas import tpu as pltpu
from jax.sharding import PartitionSpec as P

CX = 4
CY = 8
CZ = 128
NAX = 64
APER = 32
PLANES = (CX + 1) * (CY + 1)
HALF = 24
ROWS = 2 * HALF
WIDE = 2 * CZ
STEP = 8


angle_cosine = -0.6427876096865393
angle_sine = 0.766044443118978
highest = lax.Precision.HIGHEST


def with_halo(cells, sides, width):
    for axis, dim in sides:
        count = lax.axis_size(axis)
        head = lax.slice_in_dim(cells, 0, width, axis=dim)
        tail = lax.slice_in_dim(cells, cells.shape[dim] - width, cells.shape[dim], axis=dim)
        cells = jnp.concatenate(
            [
                lax.ppermute(tail, axis, [(i, (i + 1) % count) for i in range(count)]),
                cells,
                lax.ppermute(head, axis, [((i + 1) % count, i) for i in range(count)]),
            ],
            axis=dim,
        )
    return cells


def axis_table():
    counter = jnp.arange(NAX, dtype=jnp.float32) + 0.5
    height = 1.0 - 2.0 * counter / NAX
    radius = jnp.sqrt(jnp.maximum(1.0 - height * height, 0.0))
    turning = counter * 2.399963229728653
    return jnp.stack([radius * jnp.cos(turning), radius * jnp.sin(turning), height])


def rotate_about(direction, relative):
    inner_product = (
        direction[0] * relative[0] + direction[1] * relative[1] + direction[2] * relative[2]
    )
    crossed = [
        direction[1] * relative[2] - direction[2] * relative[1],
        direction[2] * relative[0] - direction[0] * relative[2],
        direction[0] * relative[1] - direction[1] * relative[0],
    ]
    return [
        relative[component] * angle_cosine
        + crossed[component] * angle_sine
        + direction[component] * inner_product * (1.0 - angle_cosine)
        for component in range(3)
    ]


def fold_rims(padded, dimension, length):
    inside = lax.slice_in_dim(padded, 1, length + 1, axis=dimension)
    lowest = lax.slice_in_dim(padded, 0, 1, axis=dimension)
    highest_rim = lax.slice_in_dim(padded, length + 1, length + 2, axis=dimension)
    position = lax.broadcasted_iota(jnp.int32, inside.shape, dimension)
    return (
        inside
        + jnp.where(position == 0, lowest, 0.0)
        + jnp.where(position == length - 1, highest_rim, 0.0)
    )


def lookup_table(rotation_axis, index_x, index_y, index_z):
    table = rotation_axis.astype(jnp.float32)
    pick_x = (index_x[:, None] == jnp.arange(APER, dtype=jnp.int32)[None, :]).astype(jnp.float32)
    pick_y = (index_y[:, None] == jnp.arange(APER, dtype=jnp.int32)[None, :]).astype(jnp.float32)
    pick_z = (index_z[:, None] == jnp.arange(APER, dtype=jnp.int32)[None, :]).astype(jnp.float32)
    section = jnp.einsum("xa,abc->xbc", pick_x, table, precision=highest)
    section = jnp.einsum("xbc,yb->xyc", section, pick_y, precision=highest)
    section = jnp.einsum("xyc,zc->xyz", section, pick_z, precision=highest)
    return (section + 0.5).astype(jnp.int32)


def pack_kernel(capacity, target_ref, velocity_ref, cell_ref, out_ref, code_ref, count_ref):
    blocks = velocity_ref.shape[0]
    devices = count_ref.shape[0]
    cell = cell_ref[...]
    plane = (cell * 8129) >> 20
    depth = cell - plane * (CZ + 1)
    inner = depth < CZ
    row = jnp.where(inner, plane, PLANES)
    lane = jnp.where(inner, depth, plane)
    upper = row >= HALF
    code_ref[...] = jnp.where(
        upper, (row - HALF) * WIDE + CZ + lane, row * WIDE + lane
    ).astype(jnp.float32)
    component = lax.broadcasted_iota(jnp.int32, out_ref.shape, 1)
    out_ref[...] = jnp.where(component == 3, -1.0, 0.0)

    def clear(d, carry):
        count_ref[d] = 0
        return carry

    lax.fori_loop(0, devices, clear, 0)

    def place(b, carry):
        target = target_ref[b]
        rank = count_ref[target]
        count_ref[target] = rank + 1
        slot = target * capacity + rank
        out_ref[slot, 0:3, :] = velocity_ref[b]
        out_ref[slot, 3:4, :] = code_ref[pl.ds(b, 1), :]
        return carry

    lax.fori_loop(0, blocks, place, 0, unroll=4)


def code_onehots(labels):
    code = labels.astype(jnp.int32)
    row = code >> 8
    column = code & (WIDE - 1)
    width = labels.shape[1]
    by_row = lax.broadcasted_iota(jnp.int32, (HALF, width), 0) == row
    by_column = lax.broadcasted_iota(jnp.int32, (WIDE, width), 0) == column
    return by_row, by_column.astype(jnp.float32).astype(jnp.bfloat16)


def scatter_kernel(x_ref, out_ref, total_ref, left_ref, right_ref):
    slots = x_ref.shape[0]
    total_ref[...] = jnp.zeros_like(total_ref)

    def step(i, carry):
        for j in range(STEP):
            data = x_ref[i * STEP + j]
            by_row, by_column = code_onehots(data[3:4])
            right_ref[:, j * CZ : (j + 1) * CZ] = by_column
            moving = data[0:3]
            upper = moving.astype(jnp.bfloat16).astype(jnp.float32)
            lower = moving - upper
            parts = [jnp.where(by_row, 1.0, 0.0)]
            for source in (upper, lower):
                for component in range(3):
                    parts.append(jnp.where(by_row, source[component : component + 1], 0.0))
            left_ref[:, j * CZ : (j + 1) * CZ] = jnp.concatenate(parts, axis=0).astype(jnp.bfloat16)
        total_ref[...] += lax.dot_general(
            left_ref[...],
            right_ref[...],
            (((1,), (1,)), ((), ())),
            preferred_element_type=jnp.float32,
        )
        return carry

    lax.fori_loop(0, slots // STEP, step, 0)
    for channel in range(4):
        value = total_ref[channel * HALF : (channel + 1) * HALF, :]
        if channel > 0:
            value = value + total_ref[(channel + 3) * HALF : (channel + 4) * HALF, :]
        out_ref[channel, 0:HALF, :] = value[:, 0:CZ]
        out_ref[channel, HALF:ROWS, :] = value[:, CZ:WIDE]


def gather_kernel(x_ref, table_ref, out_ref, held_ref):
    slots = x_ref.shape[0]
    for channel in range(6):
        value = jnp.concatenate(
            [table_ref[channel, 0:HALF, :], table_ref[channel, HALF:ROWS, :]], axis=1
        )
        upper = value.astype(jnp.bfloat16)
        held_ref[channel * HALF : (channel + 1) * HALF, :] = upper
        held_ref[(channel + 6) * HALF : (channel + 7) * HALF, :] = (
            value - upper.astype(jnp.float32)
        ).astype(jnp.bfloat16)

    def step(i, carry):
        for j in range(0, STEP, 2):
            first = i * STEP + j
            data = jnp.concatenate([x_ref[first], x_ref[first + 1]], axis=1)
            labels = data[3:4]
            by_row, by_column = code_onehots(labels)
            read = jnp.dot(held_ref[...], by_column, preferred_element_type=jnp.float32)
            picked = []
            for channel in range(6):
                value = (
                    read[channel * HALF : (channel + 1) * HALF]
                    + read[(channel + 6) * HALF : (channel + 7) * HALF]
                )
                picked.append(jnp.sum(jnp.where(by_row, value, 0.0), axis=0, keepdims=True))
            relative = [data[c : c + 1] - picked[c] for c in range(3)]
            turned = rotate_about(picked[3:], relative)
            for c in range(3):
                updated = jnp.where(labels >= 0.0, picked[c] + turned[c], 0.0)
                out_ref[first, c : c + 1, :] = updated[:, 0:CZ]
                out_ref[first + 1, c : c + 1, :] = updated[:, CZ:WIDE]
        return carry

    lax.fori_loop(0, slots // STEP, step, 0)


def local_call(kernel, out_shape, in_spaces, scratch, operations):
    return pl.pallas_call(
        kernel,
        out_shape=jax.ShapeDtypeStruct(out_shape, jnp.float32),
        in_specs=[pl.BlockSpec(memory_space=space) for space in in_spaces],
        out_specs=pl.BlockSpec(memory_space=pltpu.VMEM),
        scratch_shapes=scratch,
        cost_estimate=pl.CostEstimate(
            flops=operations, bytes_accessed=1 << 20, transcendentals=0
        ),
    )


def to_rows(cells):
    main = cells[..., :CZ].reshape(-1, PLANES, CZ)
    rim = cells[..., CZ].reshape(-1, 1, PLANES)
    rim = jnp.pad(rim, ((0, 0), (0, ROWS - PLANES - 1), (0, CZ - PLANES)))
    return jnp.concatenate([main, rim], axis=1)


def shards(velocity, cell_index, block_target, rotation_axis, grid_shift):
    devices = lax.axis_size(("gx", "gy", "gz"))
    blocks = velocity.shape[0]
    block_rows = velocity.shape[2]
    capacity = 3 * blocks // (2 * devices)
    slots = devices * capacity
    packed = local_call(
        functools.partial(pack_kernel, capacity),
        (slots, 4, block_rows),
        (pltpu.SMEM, pltpu.VMEM, pltpu.VMEM),
        [pltpu.VMEM((blocks, block_rows), jnp.float32), pltpu.SMEM((devices,), jnp.int32)],
        1 << 20,
    )(block_target[:, 0], velocity, cell_index)
    arriving = lax.all_to_all(
        packed.reshape(devices, capacity, 4, block_rows),
        ("gx", "gy", "gz"),
        split_axis=0,
        concat_axis=0,
        tiled=True,
    ).reshape(slots, 4, block_rows)
    totals = local_call(
        scatter_kernel,
        (4, ROWS, CZ),
        (pltpu.VMEM,),
        [
            pltpu.VMEM((7 * HALF, WIDE), jnp.float32),
            pltpu.VMEM((7 * HALF, STEP * CZ), jnp.bfloat16),
            pltpu.VMEM((WIDE, STEP * CZ), jnp.bfloat16),
        ],
        1 << 33,
    )(arriving)
    main = totals[:, :PLANES].reshape(4, CX + 1, CY + 1, CZ)
    rim = totals[:, PLANES, :PLANES].reshape(4, CX + 1, CY + 1, 1)
    partial_value = jnp.concatenate([main, rim], axis=3)
    folded = fold_rims(with_halo(partial_value, (("gx", 1),), 1), 1, CX + 1)
    folded = fold_rims(with_halo(folded, (("gy", 2),), 1), 2, CY + 1)
    folded = fold_rims(with_halo(folded, (("gz", 3),), 1), 3, CZ + 1)
    cell_means = folded[1:] / jnp.maximum(folded[0], 1.0)
    cell_flow = cell_means[:, :CX, :CY, :CZ]
    index_x = (
        (lax.axis_index("gx") * CX + jnp.arange(CX + 1, dtype=jnp.int32))
        % (CX * lax.axis_size("gx"))
        + grid_shift[0]
    ) % APER
    index_y = (
        (lax.axis_index("gy") * CY + jnp.arange(CY + 1, dtype=jnp.int32))
        % (CY * lax.axis_size("gy"))
        + grid_shift[1]
    ) % APER
    index_z = (
        (lax.axis_index("gz") * CZ + jnp.arange(CZ + 1, dtype=jnp.int32))
        % (CZ * lax.axis_size("gz"))
        + grid_shift[2]
    ) % APER
    picked = lookup_table(rotation_axis, index_x, index_y, index_z).reshape(-1)
    choose = (jnp.arange(NAX, dtype=jnp.int32)[:, None] == picked[None, :]).astype(jnp.float32)
    direction = jnp.dot(axis_table(), choose, precision=highest)
    table = jnp.concatenate(
        [cell_means, direction.reshape(3, CX + 1, CY + 1, CZ + 1)], axis=0
    )
    updated = local_call(
        gather_kernel,
        (slots, 3, block_rows),
        (pltpu.VMEM, pltpu.VMEM),
        [pltpu.VMEM((12 * HALF, WIDE), jnp.bfloat16)],
        1 << 33,
    )(arriving, to_rows(table))
    return (updated.reshape(1, devices, capacity, 3, block_rows), cell_flow)


def solution(mesh):
    return jax.shard_map(
        shards,
        mesh=mesh,
        in_specs=(
            P(("gx", "gy", "gz"), None, None),
            P(("gx", "gy", "gz"), None),
            P(("gx", "gy", "gz"), None),
            P(),
            P(),
        ),
        out_specs=(P(("gx", "gy", "gz"), None, None, None, None), P(None, "gx", "gy", "gz")),
        check_vma=False,
    )
```

time: 318 us -> 101 us (0.32)
  local copies, waits for them, and re-layouts: 114 us -> 9.63 us
  matrix products: 84.8 us -> 1.53 us
  other arithmetic: 64.3 us -> 3.59 us
  Pallas kernels: 0 us -> 45.6 us
  waiting for transfers between devices: 33 us -> 23 us
    dot_general x19 -> x0, matrix products: 83.2 us -> none  [the longest x8 41.7 us: add_group(): jnp.dot(weighted, depth_onehot(labels_here), precision=highest)]
    reshape x15 -> x3, local copies, waits for them, and re-layouts: 54.3 us -> 0.33 us  [the longest x2 0.3 us: shards(): direction.reshape(3, CX + 1, CY + 1, CZ + 1)]
    pallas_call x0 -> x3, Pallas kernels: none -> 45.6 us  [the longest x1 22.3 us: shards(): local_call(scatter_kernel, (4, ROWS, CZ), (pltpu.VMEM,), [pltpu.VMEM((7 *...]
    mul x8 -> x0, local copies, waits for them, and re-layouts: 39.9 us -> none  [add_group(): channels[:, None, :] * plane_onehot(labels_here, planes)[None]]
    reduce_sum x8 -> x0, other arithmetic: 33.2 us -> none  [read_group(): jnp.sum(by_depth * plane_onehot(labels_here, planes)[None], axis=1)]
    mul x8 -> x0, other arithmetic: 21.2 us -> none  [add_group(): channels[:, None, :] * plane_onehot(labels_here, planes)[None]]
    all_to_all x2 -> x1, waiting for transfers between devices: 24.8 us -> 16.4 us  [shards(): lax.all_to_all(packed.reshape(devices, capacity, 4, block_rows), ('gx', '...]
    slice x2, local copies, waits for them, and re-layouts: 8.75 us -> 1.67 us  [the longest x1 0.93 us: shards(): main = totals[:, :PLANES].reshape(4, CX + 1, CY + 1, CZ)]
  transfers between devices with their start and end apart: 8 -> 7, of which waited for: 7 -> 6; matrix products, arithmetic and copies ran while one was open for 2% -> 5% of each run, Pallas kernels for 0% -> 0%
where the time goes in v1:
time: 101 us; the launch traced here: 100 us
  Pallas kernels  45.6 us (45%)
  waiting for transfers between devices  23 us (23%)
  starting transfers between devices  16.1 us (16%)
  local copies, waits for them, and re-layouts  9.63 us (10%)
  other arithmetic  3.59 us (4%)
  matrix products  1.53 us (2%)
    pallas_call x1, Pallas kernels, shards(): local_call(scatter_kernel, (4, ROWS, CZ), (pltpu.VMEM,), [pltpu.VMEM((7 *...  22.3 us
    pallas_call x1, Pallas kernels, shards(): local_call(gather_kernel, (slots, 3, block_rows), (pltpu.VMEM, pltpu.VMEM...  19.6 us
    all_to_all x1, waiting for transfers between devices, shards(): lax.all_to_all(packed.reshape(devices, capacity, 4, block_rows), ('gx', '...  16.4 us
    all_to_all x1, starting transfers between devices, shards(): lax.all_to_all(packed.reshape(devices, capacity, 4, block_rows), ('gx', '...  7.08 us
    unnamed x9, local copies, waits for them, and re-layouts  5.73 us
    ppermute x3, starting transfers between devices, with_halo(): lax.ppermute(tail, axis, [(i, (i + 1) % count) for i in range(count)])  5.07 us
    ppermute x3, starting transfers between devices, with_halo(): lax.ppermute(head, axis, [((i + 1) % count, i) for i in range(count)])  3.95 us
    ppermute x3, waiting for transfers between devices, with_halo(): lax.ppermute(tail, axis, [(i, (i + 1) % count) for i in range(count)])  3.75 us
  transfers between devices with their start and end apart: 7, of which 6 were waited for; matrix products, arithmetic and copies ran while one was open for 5% of the time, Pallas kernels for 0%

profile of v1, /device:TPU:1, one launch (start us, length us, event | category | flops | bytes accessed | tf_op | source)
XLA Modules:
  0.0 100.3 jit_solution(17979543524128853845)
XLA Ops:
  0.6 2.1 %copy.22.velocity_ref = f32[256,3,128]{2,1,0:T(4,128)} copy(f32[256,3,128]{2,0,1:T(8,128)} %param.5) | data formatting | bytes 786432 | tf_op args[0]
  2.7 3.7 %shard_map.68 = f32[384,4,128]{2,1,0:T(4,128)} custom-call(s32[256]{0:T(256)} %bitcast.57, f32[256,3,128]{2,1,0:T(4,128)} %copy.22.velocity_ref, s32[256,128]{1,0:T(8,128)} %cell_ref.1), custom_call_target="tpu_custom_call" | custom-call | flops 1048576 | bytes 1048576 | tf_op jit(solution)/shard_map/pallas_call | solution.py:231
  6.4 7.1 %all-to-all-start = ((f32[32,12,4,128]{3,2,1,0:T(4,128)}), f32[32,12,4,128]{3,2,1,0:T(4,128)S(1)}, u32[]{:S(2)}, u32[]{:S(2)}) async-start(f32[32,12,4,128]{3,2,1,0:T(4,128)} %bitcast.34), calls=%async_computation | async-start | bytes 1572864 | tf_op jit(solution)/shard_map/all_to_all | solution.py:238
  13.5 0.6 fusion.39
  14.1 0.7 and_select_fusion.4
  14.8 0.6 and_select_fusion.2
  15.4 0.7 and_select_fusion
  16.0 0.6 fusion.3
  16.6 0.2 convolution_bitcast_fusion
  17.2 0.6 fusion
  17.8 16.4 %all-to-all-done = f32[32,12,4,128]{3,2,1,0:T(4,128)S(1)} async-done(((f32[32,12,4,128]{3,2,1,0:T(4,128)}), f32[32,12,4,128]{3,2,1,0:T(4,128)S(1)}, u32[]{:S(2)}, u32[]{:S(2)}) %all-to-all-start) | async-done | bytes 786464 | tf_op jit(solution)/shard_map/all_to_all | solution.py:238
  34.3 0.9 copy-done
  35.1 22.3 %shard_map.69 = f32[4,48,128]{2,1,0:T(8,128)} custom-call(f32[384,4,128]{2,1,0:T(4,128)} %bitcast.39), custom_call_target="tpu_custom_call" | custom-call | flops 8589934592 | bytes 1048576 | tf_op jit(solution)/shard_map/pallas_call | solution.py:245
  57.5 0.7 slice_reduce_fusion
  58.3 0.2 copy.24
  58.5 0.9 copy.23
  59.5 0.8 collective-permute-start
  60.3 0.7 collective-permute-start.1
  61.0 1.3 %collective-permute-done = f32[4,1,9,129]{3,0,2,1:T(4,128)S(1)} collective-permute-done((f32[4,1,9,129]{3,0,2,1:T(4,128)S(1)}, f32[4,1,9,129]{3,0,2,1:T(4,128)S(1)}, u32[]{:S(2)}, u32[]{:S(2)}) %collective-permute-start) | collective-permute-done | bytes 18608 | tf_op jit(solution)/shard_map/ppermute | solution.py:33
  62.3 0.8 collective-permute-done.1
  63.4 3.3 %collective-permute-start.3 = (f32[4,5,1,129]{3,0,2,1:T(4,128)S(1)}, f32[4,5,1,129]{3,0,2,1:T(4,128)S(1)}, u32[]{:S(2)}, u32[]{:S(2)}) collective-permute-start(f32[4,5,1,129]{3,0,2,1:T(4,128)S(1)} %get-tuple-element.11), channel_id=1, source_target_pairs={{4,0},{8,4},{12,8},{0,12},{5,1},{9,5},{13,9},{1,13},{6,2},{10,6},{... | collective-permute-start | bytes 30968 | tf_op jit(solution)/shard_map/ppermute | solution.py:35
  66.6 1.2 %collective-permute-done.2 = f32[4,5,1,129]{3,0,2,1:T(4,128)S(1)} collective-permute-done((f32[4,5,1,129]{3,0,2,1:T(4,128)S(1)}, f32[4,5,1,129]{3,0,2,1:T(4,128)S(1)}, u32[]{:S(2)}, u32[]{:S(2)}) %collective-permute-start.2) | collective-permute-done | bytes 10352 | tf_op jit(solution)/shard_map/ppermute | solution.py:33
  68.0 4.2 %collective-permute-start.4 = (f32[4,5,9,1]{3,0,2,1:T(4,128)S(1)}, f32[4,5,9,1]{3,0,2,1:T(4,128)S(1)}, u32[]{:S(2)}, u32[]{:S(2)}) collective-permute-start(f32[4,5,9,1]{3,0,2,1:T(4,128)S(1)} %get-tuple-element.8), channel_id=1, source_target_pairs={{0,1},{1,2},{2,3},{3,0},{4,5},{5,6},{6,7},{7,4},{8,9},{9,10},{10,1... | collective-permute-start | bytes 2168 | tf_op jit(solution)/shard_map/ppermute | solution.py:33
  72.5 1.3 %collective-permute-done.4 = f32[4,5,9,1]{3,0,2,1:T(4,128)S(1)} collective-permute-done((f32[4,5,9,1]{3,0,2,1:T(4,128)S(1)}, f32[4,5,9,1]{3,0,2,1:T(4,128)S(1)}, u32[]{:S(2)}, u32[]{:S(2)}) %collective-permute-start.4) | collective-permute-done | bytes 752 | tf_op jit(solution)/shard_map/ppermute | solution.py:33
  73.8 0.2 copy.25
  74.1 2.0 %collective-permute-done.5 = f32[4,5,9,1]{3,0,2,1:T(4,128)S(1)} collective-permute-done((f32[4,5,9,1]{3,0,2,1:T(4,128)S(1)}, f32[4,5,9,1]{3,0,2,1:T(4,128)S(1)}, u32[]{:S(2)}, u32[]{:S(2)}) %collective-permute-start.5) | collective-permute-done | bytes 752 | tf_op jit(solution)/shard_map/ppermute | solution.py:35
  76.2 0.2 copy.27
  76.5 0.2 select_add_fusion
  77.1 0.6 copy.37
  77.9 0.7 select_maximum_fusion.table_ref
  78.5 19.6 %shard_map.70 = f32[384,3,128]{2,1,0:T(4,128)} custom-call(f32[384,4,128]{2,1,0:T(4,128)} %bitcast.40, f32[6,48,128]{2,1,0:T(8,128)} %select_maximum_fusion.table_ref), custom_call_target="tpu_custom_call" | custom-call | flops 8589934592 | bytes 1048576 | tf_op jit(solution)/shard_map/pallas_call | solution.py:285
  98.1 2.1 %copy.36 = f32[1,32,12,3,128]{4,1,3,2,0:T(8,128)} copy(f32[1,32,12,3,128]{4,3,2,1,0:T(4,128)} %bitcast.41) | data formatting | bytes 1179648
  (35 shorter events, 2.0 us)
Async XLA Ops:
  6.4 7.1 %copy-start.2 = (s32[3]{0:T(128)S(1)}, s32[3]{0:T(128)}, u32[]{:S(2)}) copy-start(s32[3]{0:T(128)} %param.9) | copy-start | bytes 40
  6.4 7.7 %copy-start.1 = (s32[32,32,32]{2,1,0:T(8,128)S(1)}, s32[32,32,32]{2,1,0:T(8,128)}, u32[]{:S(2)}) copy-start(s32[32,32,32]{2,1,0:T(8,128)} %param.8) | copy-start | bytes 393220
  6.4 27.9 %all-to-all-start = ((f32[32,12,4,128]{3,2,1,0:T(4,128)}), f32[32,12,4,128]{3,2,1,0:T(4,128)S(1)}, u32[]{:S(2)}, u32[]{:S(2)}) async-start(f32[32,12,4,128]{3,2,1,0:T(4,128)} %bitcast.34), calls=%async_computation | async-start | bytes 1572864 | tf_op jit(solution)/shard_map/all_to_all | solution.py:238
  34.2 0.9 copy-start
  59.5 2.9 %collective-permute-start = (f32[4,1,9,129]{3,0,2,1:T(4,128)S(1)}, f32[4,1,9,129]{3,0,2,1:T(4,128)S(1)}, u32[]{:S(2)}, u32[]{:S(2)}) collective-permute-start(f32[4,1,9,129]{3,0,2,1:T(4,128)S(1)} %get-tuple-element.12), channel_id=1, source_target_pairs={{0,16},{16,0},{1,17},{17,1},{2,18},{18,2},{3,19},{19,3},{4,20},{20... | collective-permute-start | bytes 55736 | tf_op jit(solution)/shard_map/ppermute | solution.py:33
  60.3 2.8 %collective-permute-start.1 = (f32[4,1,9,129]{3,0,2,1:T(4,128)S(1)}, f32[4,1,9,129]{3,0,2,1:T(4,128)S(1)}, u32[]{:S(2)}, u32[]{:S(2)}) collective-permute-start(f32[4,1,9,129]{3,0,2,1:T(4,128)S(1)} %get-tuple-element.13), channel_id=1, source_target_pairs={{16,0},{0,16},{17,1},{1,17},{18,2},{2,18},{19,3},{3,19},{20,4},{4,... | collective-permute-start | bytes 55736 | tf_op jit(solution)/shard_map/ppermute | solution.py:35
  63.3 4.5 %collective-permute-start.2 = (f32[4,5,1,129]{3,0,2,1:T(4,128)S(1)}, f32[4,5,1,129]{3,0,2,1:T(4,128)S(1)}, u32[]{:S(2)}, u32[]{:S(2)}) collective-permute-start(f32[4,5,1,129]{3,0,2,1:T(4,128)S(1)} %get-tuple-element.10), channel_id=1, source_target_pairs={{0,4},{4,8},{8,12},{12,0},{1,5},{5,9},{9,13},{13,1},{2,6},{6,10},{... | collective-permute-start | bytes 30968 | tf_op jit(solution)/shard_map/ppermute | solution.py:33
  63.4 4.4 %collective-permute-start.3 = (f32[4,5,1,129]{3,0,2,1:T(4,128)S(1)}, f32[4,5,1,129]{3,0,2,1:T(4,128)S(1)}, u32[]{:S(2)}, u32[]{:S(2)}) collective-permute-start(f32[4,5,1,129]{3,0,2,1:T(4,128)S(1)} %get-tuple-element.11), channel_id=1, source_target_pairs={{4,0},{8,4},{12,8},{0,12},{5,1},{9,5},{13,9},{1,13},{6,2},{10,6},{... | collective-permute-start | bytes 30968 | tf_op jit(solution)/shard_map/ppermute | solution.py:35
  68.0 5.8 %collective-permute-start.4 = (f32[4,5,9,1]{3,0,2,1:T(4,128)S(1)}, f32[4,5,9,1]{3,0,2,1:T(4,128)S(1)}, u32[]{:S(2)}, u32[]{:S(2)}) collective-permute-start(f32[4,5,9,1]{3,0,2,1:T(4,128)S(1)} %get-tuple-element.8), channel_id=1, source_target_pairs={{0,1},{1,2},{2,3},{3,0},{4,5},{5,6},{6,7},{7,4},{8,9},{9,10},{10,1... | collective-permute-start | bytes 2168 | tf_op jit(solution)/shard_map/ppermute | solution.py:33
  72.2 4.0 %collective-permute-start.5 = (f32[4,5,9,1]{3,0,2,1:T(4,128)S(1)}, f32[4,5,9,1]{3,0,2,1:T(4,128)S(1)}, u32[]{:S(2)}, u32[]{:S(2)}) collective-permute-start(f32[4,5,9,1]{3,0,2,1:T(4,128)S(1)} %get-tuple-element.9), channel_id=1, source_target_pairs={{1,0},{2,1},{3,2},{0,3},{5,4},{6,5},{7,6},{4,7},{9,8},{10,9},{11,1... | collective-permute-start | bytes 2168 | tf_op jit(solution)/shard_map/ppermute | solution.py:35

commit v2 on v1

--- a/solution.py
+++ b/solution.py
@@ -87,8 +87,8 @@
     return (section + 0.5).astype(jnp.int32)
 
 
-def pack_kernel(capacity, target_ref, velocity_ref, cell_ref, out_ref, code_ref, count_ref):
-    blocks = velocity_ref.shape[0]
+def pack_kernel(sizes, target_ref, velocity_ref, cell_ref, first_ref, second_ref, code_ref, count_ref):
+    blocks = velocity_ref.shape[1]
     devices = count_ref.shape[0]
     cell = cell_ref[...]
     plane = (cell * 8129) >> 20
@@ -100,8 +100,9 @@
     code_ref[...] = jnp.where(
         upper, (row - HALF) * WIDE + CZ + lane, row * WIDE + lane
     ).astype(jnp.float32)
-    component = lax.broadcasted_iota(jnp.int32, out_ref.shape, 1)
-    out_ref[...] = jnp.where(component == 3, -1.0, 0.0)
+    for out_ref in (first_ref, second_ref):
+        component = lax.broadcasted_iota(jnp.int32, out_ref.shape, 1)
+        out_ref[...] = jnp.where(component == 3, -1.0, 0.0)
 
     def clear(d, carry):
         count_ref[d] = 0
@@ -113,9 +114,20 @@
         target = target_ref[b]
         rank = count_ref[target]
         count_ref[target] = rank + 1
-        slot = target * capacity + rank
-        out_ref[slot, 0:3, :] = velocity_ref[b]
-        out_ref[slot, 3:4, :] = code_ref[pl.ds(b, 1), :]
+
+        def put(out_ref, slot):
+            for component in range(3):
+                out_ref[slot, component : component + 1, :] = velocity_ref[component, pl.ds(b, 1), :]
+            out_ref[slot, 3:4, :] = code_ref[pl.ds(b, 1), :]
+
+        @pl.when(rank < sizes[0])
+        def early():
+            put(first_ref, target * sizes[0] + rank)
+
+        @pl.when(rank >= sizes[0])
+        def late():
+            put(second_ref, target * sizes[1] + rank - sizes[0])
+
         return carry
 
     lax.fori_loop(0, blocks, place, 0, unroll=4)
@@ -131,9 +143,12 @@
     return by_row, by_column.astype(jnp.float32).astype(jnp.bfloat16)
 
 
-def scatter_kernel(x_ref, out_ref, total_ref, left_ref, right_ref):
+def scatter_kernel(x_ref, before_ref, out_ref, total_ref, left_ref, right_ref):
     slots = x_ref.shape[0]
-    total_ref[...] = jnp.zeros_like(total_ref)
+    for channel in range(4):
+        total_ref[channel * HALF : (channel + 1) * HALF, 0:CZ] = before_ref[channel, 0:HALF, :]
+        total_ref[channel * HALF : (channel + 1) * HALF, CZ:WIDE] = before_ref[channel, HALF:ROWS, :]
+    total_ref[4 * HALF : 7 * HALF, :] = jnp.zeros((3 * HALF, WIDE), jnp.float32)
 
     def step(i, carry):
         for j in range(STEP):
@@ -165,8 +180,9 @@
         out_ref[channel, HALF:ROWS, :] = value[:, CZ:WIDE]
 
 
-def gather_kernel(x_ref, table_ref, out_ref, held_ref):
-    slots = x_ref.shape[0]
+def gather_kernel(sizes, first_ref, second_ref, table_ref, out_ref, held_ref):
+    devices = out_ref.shape[2]
+    groups = devices // STEP
     for channel in range(6):
         value = jnp.concatenate(
             [table_ref[channel, 0:HALF, :], table_ref[channel, HALF:ROWS, :]], axis=1
@@ -177,37 +193,48 @@
             value - upper.astype(jnp.float32)
         ).astype(jnp.bfloat16)
 
-    def step(i, carry):
-        for j in range(0, STEP, 2):
-            first = i * STEP + j
-            data = jnp.concatenate([x_ref[first], x_ref[first + 1]], axis=1)
-            labels = data[3:4]
-            by_row, by_column = code_onehots(labels)
-            read = jnp.dot(held_ref[...], by_column, preferred_element_type=jnp.float32)
-            picked = []
-            for channel in range(6):
-                value = (
-                    read[channel * HALF : (channel + 1) * HALF]
-                    + read[(channel + 6) * HALF : (channel + 7) * HALF]
+    def read_from(x_ref, size, offset):
+        def step(i, carry):
+            rank = i // groups
+            sender = (i % groups) * STEP
+            blocks = [x_ref[(sender + j) * size + rank] for j in range(STEP)]
+            picked = [[] for channel in range(6)]
+            for j in range(0, STEP, 2):
+                labels = jnp.concatenate([blocks[j][3:4], blocks[j + 1][3:4]], axis=1)
+                by_row, by_column = code_onehots(labels)
+                read = jnp.dot(held_ref[...], by_column, preferred_element_type=jnp.float32)
+                for channel in range(6):
+                    value = (
+                        read[channel * HALF : (channel + 1) * HALF]
+                        + read[(channel + 6) * HALF : (channel + 7) * HALF]
+                    )
+                    row = jnp.sum(jnp.where(by_row, value, 0.0), axis=0, keepdims=True)
+                    picked[channel] += [row[:, 0:CZ], row[:, CZ:WIDE]]
+            held = [jnp.concatenate(rows, axis=0) for rows in picked]
+            own = [
+                jnp.concatenate([block[c : c + 1] for block in blocks], axis=0) for c in range(4)
+            ]
+            relative = [own[c] - held[c] for c in range(3)]
+            turned = rotate_about(held[3:], relative)
+            place = pl.ds(pl.multiple_of(sender, STEP), STEP)
+            for c in range(3):
+                out_ref[offset + rank, c, place, :] = jnp.where(
+                    own[3] >= 0.0, held[c] + turned[c], 0.0
                 )
-                picked.append(jnp.sum(jnp.where(by_row, value, 0.0), axis=0, keepdims=True))
-            relative = [data[c : c + 1] - picked[c] for c in range(3)]
-            turned = rotate_about(picked[3:], relative)
-            for c in range(3):
-                updated = jnp.where(labels >= 0.0, picked[c] + turned[c], 0.0)
-                out_ref[first, c : c + 1, :] = updated[:, 0:CZ]
-                out_ref[first + 1, c : c + 1, :] = updated[:, CZ:WIDE]
-        return carry
-
-    lax.fori_loop(0, slots // STEP, step, 0)
+            return carry
+
+        lax.fori_loop(0, size * groups, step, 0)
+
+    read_from(first_ref, sizes[0], 0)
+    read_from(second_ref, sizes[1], sizes[0])
 
 
 def local_call(kernel, out_shape, in_spaces, scratch, operations):
     return pl.pallas_call(
         kernel,
-        out_shape=jax.ShapeDtypeStruct(out_shape, jnp.float32),
+        out_shape=[jax.ShapeDtypeStruct(shape, jnp.float32) for shape in out_shape],
         in_specs=[pl.BlockSpec(memory_space=space) for space in in_spaces],
-        out_specs=pl.BlockSpec(memory_space=pltpu.VMEM),
+        out_specs=[pl.BlockSpec(memory_space=pltpu.VMEM) for shape in out_shape],
         scratch_shapes=scratch,
         cost_estimate=pl.CostEstimate(
             flops=operations, bytes_accessed=1 << 20, transcendentals=0
@@ -227,32 +254,38 @@
     blocks = velocity.shape[0]
     block_rows = velocity.shape[2]
     capacity = 3 * blocks // (2 * devices)
-    slots = devices * capacity
+    sizes = (capacity // 2, capacity - capacity // 2)
     packed = local_call(
-        functools.partial(pack_kernel, capacity),
-        (slots, 4, block_rows),
+        functools.partial(pack_kernel, sizes),
+        [(devices * size, 4, block_rows) for size in sizes],
         (pltpu.SMEM, pltpu.VMEM, pltpu.VMEM),
         [pltpu.VMEM((blocks, block_rows), jnp.float32), pltpu.SMEM((devices,), jnp.int32)],
         1 << 20,
-    )(block_target[:, 0], velocity, cell_index)
-    arriving = lax.all_to_all(
-        packed.reshape(devices, capacity, 4, block_rows),
-        ("gx", "gy", "gz"),
-        split_axis=0,
-        concat_axis=0,
-        tiled=True,
-    ).reshape(slots, 4, block_rows)
-    totals = local_call(
-        scatter_kernel,
-        (4, ROWS, CZ),
-        (pltpu.VMEM,),
-        [
-            pltpu.VMEM((7 * HALF, WIDE), jnp.float32),
-            pltpu.VMEM((7 * HALF, STEP * CZ), jnp.bfloat16),
-            pltpu.VMEM((WIDE, STEP * CZ), jnp.bfloat16),
-        ],
-        1 << 33,
-    )(arriving)
+    )(block_target[:, 0], jnp.transpose(velocity, (1, 0, 2)), cell_index)
+    arrived = []
+    totals = jnp.zeros((4, ROWS, CZ), jnp.float32)
+    for size, outgoing in zip(sizes, packed):
+        arrived.append(
+            lax.all_to_all(
+                outgoing.reshape(devices, size, 4, block_rows),
+                ("gx", "gy", "gz"),
+                split_axis=0,
+                concat_axis=0,
+                tiled=True,
+            ).reshape(devices * size, 4, block_rows)
+        )
+    for arriving in arrived:
+        totals = local_call(
+            scatter_kernel,
+            [(4, ROWS, CZ)],
+            (pltpu.VMEM, pltpu.VMEM),
+            [
+                pltpu.VMEM((7 * HALF, WIDE), jnp.float32),
+                pltpu.VMEM((7 * HALF, STEP * CZ), jnp.bfloat16),
+                pltpu.VMEM((WIDE, STEP * CZ), jnp.bfloat16),
+            ],
+            1 << 33,
+        )(arriving, totals)[0]
     main = totals[:, :PLANES].reshape(4, CX + 1, CY + 1, CZ)
     rim = totals[:, PLANES, :PLANES].reshape(4, CX + 1, CY + 1, 1)
     partial_value = jnp.concatenate([main, rim], axis=3)
@@ -283,13 +316,13 @@
         [cell_means, direction.reshape(3, CX + 1, CY + 1, CZ + 1)], axis=0
     )
     updated = local_call(
-        gather_kernel,
-        (slots, 3, block_rows),
-        (pltpu.VMEM, pltpu.VMEM),
+        functools.partial(gather_kernel, sizes),
+        [(capacity, 3, devices, block_rows)],
+        (pltpu.VMEM, pltpu.VMEM, pltpu.VMEM),
         [pltpu.VMEM((12 * HALF, WIDE), jnp.bfloat16)],
         1 << 33,
-    )(arriving, to_rows(table))
-    return (updated.reshape(1, devices, capacity, 3, block_rows), cell_flow)
+    )(*arrived, to_rows(table))[0]
+    return (jnp.transpose(updated, (2, 0, 1, 3))[None], cell_flow)
 
 
 def solution(mesh):

time: 101 us -> 96.6 us (0.956)
  waiting for transfers between devices: 23 us -> 16.1 us
  Pallas kernels: 45.6 us -> 49.8 us
  local copies, waits for them, and re-layouts: 9.63 us -> 5.96 us
  starting transfers between devices: 16.1 us -> 18.3 us
    all_to_all x1 -> x2, waiting for transfers between devices: 16.4 us -> 8.32 us  [shards(): lax.all_to_all(outgoing.reshape(devices, size, 4, block_rows), ('gx', 'gy...]
    unnamed x9, local copies, waits for them, and re-layouts: 5.73 us -> 1.39 us
    pallas_call x3 -> x4, Pallas kernels: 45.6 us -> 49.8 us  [the longest x2 23.9 us: shards(): local_call(scatter_kernel, [(4, ROWS, CZ)], (pltpu.VMEM, pltpu.VMEM), [pl...]
    all_to_all x1 -> x2, starting transfers between devices: 7.08 us -> 10.1 us  [shards(): lax.all_to_all(outgoing.reshape(devices, size, 4, block_rows), ('gx', 'gy...]
    ppermute x3, waiting for transfers between devices: 2.82 us -> 3.98 us  [with_halo(): lax.ppermute(head, axis, [((i + 1) % count, i) for i in range(count)])]
    ppermute x3, starting transfers between devices: 3.95 us -> 2.87 us  [with_halo(): lax.ppermute(head, axis, [((i + 1) % count, i) for i in range(count)])]
  transfers between devices with their start and end apart: 7 -> 8, of which waited for: 6 -> 7; matrix products, arithmetic and copies ran while one was open for 5% -> 6% of each run, Pallas kernels for 0% -> 12%
where the time goes in v2:
time: 96.6 us; the launch traced here: 96.1 us
  Pallas kernels  49.8 us (52%)
  starting transfers between devices  18.3 us (19%)
  waiting for transfers between devices  16.1 us (17%)
  local copies, waits for them, and re-layouts  5.96 us (6%)
  other arithmetic  3.59 us (4%)
  matrix products  1.53 us (2%)
    pallas_call x2, Pallas kernels, shards(): local_call(scatter_kernel, [(4, ROWS, CZ)], (pltpu.VMEM, pltpu.VMEM), [pl...  23.9 us
    pallas_call x1, Pallas kernels, shards(): local_call(functools.partial(gather_kernel, sizes), [(capacity, 3, device...  18.8 us
    all_to_all x2, starting transfers between devices, shards(): lax.all_to_all(outgoing.reshape(devices, size, 4, block_rows), ('gx', 'gy...  10.1 us
    all_to_all x2, waiting for transfers between devices, shards(): lax.all_to_all(outgoing.reshape(devices, size, 4, block_rows), ('gx', 'gy...  8.32 us
    pallas_call x1, Pallas kernels, shards(): local_call(functools.partial(pack_kernel, sizes), [(devices * size, 4, bl...  7.12 us
    ppermute x3, starting transfers between devices, with_halo(): lax.ppermute(tail, axis, [(i, (i + 1) % count) for i in range(count)])  5.41 us
    ppermute x3, waiting for transfers between devices, with_halo(): lax.ppermute(head, axis, [((i + 1) % count, i) for i in range(count)])  3.98 us
    ppermute x3, waiting for transfers between devices, with_halo(): lax.ppermute(tail, axis, [(i, (i + 1) % count) for i in range(count)])  3.75 us
  transfers between devices with their start and end apart: 8, of which 7 were waited for; matrix products, arithmetic and copies ran while one was open for 6% of the time, Pallas kernels for 12%

profile of v2, /device:TPU:1, one launch (start us, length us, event | category | flops | bytes accessed | tf_op | source)
XLA Modules:
  0.0 96.1 jit_solution(16826655413395989124)
XLA Ops:
  0.7 7.1 %shard_map.68 = (f32[192,4,128]{2,1,0:T(4,128)}, f32[192,4,128]{2,1,0:T(4,128)}) custom-call(s32[256]{0:T(256)} %bitcast.64, f32[3,256,128]{2,1,0:T(8,128)} %bitcast.49, s32[256,128]{1,0:T(8,128)} %cell_ref.1), custom_call_target="tpu_custom_call" | custom-call | flops 1048576 | bytes 1048576 | tf_op jit(solution)/shard_map/pallas_call | solution.py:258
  7.8 7.1 %all-to-all-start = ((f32[32,6,4,128]{3,2,1,0:T(4,128)}), f32[32,6,4,128]{3,2,1,0:T(4,128)S(1)}, u32[]{:S(2)}, u32[]{:S(2)}) async-start(f32[32,6,4,128]{3,2,1,0:T(4,128)} %bitcast.48), calls=%async_computation | async-start | bytes 786432 | tf_op jit(solution)/shard_map/all_to_all | solution.py:269
  14.9 0.6 fusion.39
  15.5 0.7 and_select_fusion.4
  16.2 0.6 and_select_fusion.2
  16.8 0.6 fusion.3
  17.6 0.7 and_select_fusion
  18.7 0.6 fusion
  19.2 8.2 %all-to-all-done = f32[32,6,4,128]{3,2,1,0:T(4,128)S(1)} async-done(((f32[32,6,4,128]{3,2,1,0:T(4,128)}), f32[32,6,4,128]{3,2,1,0:T(4,128)S(1)}, u32[]{:S(2)}, u32[]{:S(2)}) %all-to-all-start) | async-done | bytes 393248 | tf_op jit(solution)/shard_map/all_to_all | solution.py:269
  27.4 3.0 %all-to-all-start.1 = ((f32[32,6,4,128]{3,2,1,0:T(4,128)}), f32[32,6,4,128]{3,2,1,0:T(4,128)S(1)}, u32[]{:S(2)}, u32[]{:S(2)}) async-start(f32[32,6,4,128]{3,2,1,0:T(4,128)} %bitcast.4), calls=%async_computation.1 | async-start | bytes 786432 | tf_op jit(solution)/shard_map/all_to_all | solution.py:269
  30.4 0.6 broadcast_in_dim.76.before_ref
  31.1 11.9 %shard_map.69.before_ref = f32[4,48,128]{2,1,0:T(8,128)} custom-call(f32[192,4,128]{2,1,0:T(4,128)} %bitcast.44, f32[4,48,128]{2,1,0:T(8,128)} %broadcast_in_dim.76.before_ref), custom_call_target="tpu_custom_call" | custom-call | flops 8589934592 | bytes 1048576 | tf_op jit(solution)/shard_map/pallas_call | solution.py:278
  43.1 0.8 copy-done.2
  43.9 11.9 %shard_map.70 = f32[4,48,128]{2,1,0:T(8,128)} custom-call(f32[192,4,128]{2,1,0:T(4,128)} %bitcast.46, f32[4,48,128]{2,1,0:T(8,128)} %shard_map.69.before_ref), custom_call_target="tpu_custom_call" | custom-call | flops 8589934592 | bytes 1048576 | tf_op jit(solution)/shard_map/pallas_call | solution.py:278
  55.8 0.7 slice_reduce_fusion
  56.6 0.2 copy.19
  56.9 0.9 copy.18
  57.8 1.3 %collective-permute-start = (f32[4,1,9,129]{3,0,2,1:T(4,128)S(1)}, f32[4,1,9,129]{3,0,2,1:T(4,128)S(1)}, u32[]{:S(2)}, u32[]{:S(2)}) collective-permute-start(f32[4,1,9,129]{3,0,2,1:T(4,128)S(1)} %get-tuple-element.14), channel_id=1, source_target_pairs={{0,16},{16,0},{1,17},{17,1},{2,18},{18,2},{3,19},{19,3},{4,20},{20... | collective-permute-start | bytes 55736 | tf_op jit(solution)/shard_map/ppermute | solution.py:33
  59.4 1.3 %collective-permute-done = f32[4,1,9,129]{3,0,2,1:T(4,128)S(1)} collective-permute-done((f32[4,1,9,129]{3,0,2,1:T(4,128)S(1)}, f32[4,1,9,129]{3,0,2,1:T(4,128)S(1)}, u32[]{:S(2)}, u32[]{:S(2)}) %collective-permute-start) | collective-permute-done | bytes 18608 | tf_op jit(solution)/shard_map/ppermute | solution.py:33
  60.7 1.9 %collective-permute-done.1 = f32[4,1,9,129]{3,0,2,1:T(4,128)S(1)} collective-permute-done((f32[4,1,9,129]{3,0,2,1:T(4,128)S(1)}, f32[4,1,9,129]{3,0,2,1:T(4,128)S(1)}, u32[]{:S(2)}, u32[]{:S(2)}) %collective-permute-start.1) | collective-permute-done | bytes 18608 | tf_op jit(solution)/shard_map/ppermute | solution.py:35
  62.8 0.7 collective-permute-start.2
  63.5 2.7 %collective-permute-start.3 = (f32[4,5,1,129]{3,0,2,1:T(4,128)S(1)}, f32[4,5,1,129]{3,0,2,1:T(4,128)S(1)}, u32[]{:S(2)}, u32[]{:S(2)}) collective-permute-start(f32[4,5,1,129]{3,0,2,1:T(4,128)S(1)} %get-tuple-element.13), channel_id=1, source_target_pairs={{4,0},{8,4},{12,8},{0,12},{5,1},{9,5},{13,9},{1,13},{6,2},{10,6},{... | collective-permute-start | bytes 30968 | tf_op jit(solution)/shard_map/ppermute | solution.py:35
  66.1 1.2 %collective-permute-done.2 = f32[4,5,1,129]{3,0,2,1:T(4,128)S(1)} collective-permute-done((f32[4,5,1,129]{3,0,2,1:T(4,128)S(1)}, f32[4,5,1,129]{3,0,2,1:T(4,128)S(1)}, u32[]{:S(2)}, u32[]{:S(2)}) %collective-permute-start.2) | collective-permute-done | bytes 10352 | tf_op jit(solution)/shard_map/ppermute | solution.py:33
  67.5 3.4 %collective-permute-start.4 = (f32[4,5,9,1]{3,0,2,1:T(4,128)S(1)}, f32[4,5,9,1]{3,0,2,1:T(4,128)S(1)}, u32[]{:S(2)}, u32[]{:S(2)}) collective-permute-start(f32[4,5,9,1]{3,0,2,1:T(4,128)S(1)} %get-tuple-element.10), channel_id=1, source_target_pairs={{0,1},{1,2},{2,3},{3,0},{4,5},{5,6},{6,7},{7,4},{8,9},{9,10},{10,1... | collective-permute-start | bytes 2168 | tf_op jit(solution)/shard_map/ppermute | solution.py:33
  71.3 1.3 %collective-permute-done.4 = f32[4,5,9,1]{3,0,2,1:T(4,128)S(1)} collective-permute-done((f32[4,5,9,1]{3,0,2,1:T(4,128)S(1)}, f32[4,5,9,1]{3,0,2,1:T(4,128)S(1)}, u32[]{:S(2)}, u32[]{:S(2)}) %collective-permute-start.4) | collective-permute-done | bytes 752 | tf_op jit(solution)/shard_map/ppermute | solution.py:33
  72.5 0.2 copy.20
  72.9 2.0 %collective-permute-done.5 = f32[4,5,9,1]{3,0,2,1:T(4,128)S(1)} collective-permute-done((f32[4,5,9,1]{3,0,2,1:T(4,128)S(1)}, f32[4,5,9,1]{3,0,2,1:T(4,128)S(1)}, u32[]{:S(2)}, u32[]{:S(2)}) %collective-permute-start.5) | collective-permute-done | bytes 752 | tf_op jit(solution)/shard_map/ppermute | solution.py:35
  74.9 0.2 copy.22
  75.3 0.2 select_add_fusion
  76.0 0.6 copy.31
  76.6 0.7 select_maximum_fusion.table_ref
  77.3 18.8 %shard_map.71 = f32[12,3,32,128]{3,2,1,0:T(8,128)} custom-call(f32[192,4,128]{2,1,0:T(4,128)} %bitcast.45, f32[192,4,128]{2,1,0:T(4,128)} %bitcast.47, f32[6,48,128]{2,1,0:T(8,128)} %select_maximum_fusion.table_ref), custom_call_target="tpu_custom_call" | custom-call | flops 8589934592 | bytes 1048576 | tf_op jit(solution)/shard_map/pallas_call | solution.py:318
  (39 shorter events, 2.5 us)
Async XLA Ops:
  0.6 14.2 %copy-start.3 = (s32[3]{0:T(128)S(1)}, s32[3]{0:T(128)}, u32[]{:S(2)}) copy-start(s32[3]{0:T(128)} %param.9) | copy-start | bytes 40
  0.6 14.9 %copy-start = (s32[32,32,32]{2,1,0:T(8,128)S(1)}, s32[32,32,32]{2,1,0:T(8,128)}, u32[]{:S(2)}) copy-start(s32[32,32,32]{2,1,0:T(8,128)} %param.8) | copy-start | bytes 393220
  7.8 19.7 %all-to-all-start = ((f32[32,6,4,128]{3,2,1,0:T(4,128)}), f32[32,6,4,128]{3,2,1,0:T(4,128)S(1)}, u32[]{:S(2)}, u32[]{:S(2)}) async-start(f32[32,6,4,128]{3,2,1,0:T(4,128)} %bitcast.48), calls=%async_computation | async-start | bytes 786432 | tf_op jit(solution)/shard_map/all_to_all | solution.py:269
  27.4 3.6 %copy-start.1 = (f32[32,6,4,128]{3,2,1,0:T(4,128)}, f32[32,6,4,128]{3,2,1,0:T(4,128)S(1)}, u32[]{:S(2)}) copy-start(f32[32,6,4,128]{3,2,1,0:T(4,128)S(1)} %all-to-all-done) | copy-start | bytes 1179652
  27.4 15.7 %all-to-all-start.1 = ((f32[32,6,4,128]{3,2,1,0:T(4,128)}), f32[32,6,4,128]{3,2,1,0:T(4,128)S(1)}, u32[]{:S(2)}, u32[]{:S(2)}) async-start(f32[32,6,4,128]{3,2,1,0:T(4,128)} %bitcast.4), calls=%async_computation.1 | async-start | bytes 786432 | tf_op jit(solution)/shard_map/all_to_all | solution.py:269
  43.1 0.8 copy-start.2
  57.8 2.9 %collective-permute-start = (f32[4,1,9,129]{3,0,2,1:T(4,128)S(1)}, f32[4,1,9,129]{3,0,2,1:T(4,128)S(1)}, u32[]{:S(2)}, u32[]{:S(2)}) collective-permute-start(f32[4,1,9,129]{3,0,2,1:T(4,128)S(1)} %get-tuple-element.14), channel_id=1, source_target_pairs={{0,16},{16,0},{1,17},{17,1},{2,18},{18,2},{3,19},{19,3},{4,20},{20... | collective-permute-start | bytes 55736 | tf_op jit(solution)/shard_map/ppermute | solution.py:33
  59.2 3.5 %collective-permute-start.1 = (f32[4,1,9,129]{3,0,2,1:T(4,128)S(1)}, f32[4,1,9,129]{3,0,2,1:T(4,128)S(1)}, u32[]{:S(2)}, u32[]{:S(2)}) collective-permute-start(f32[4,1,9,129]{3,0,2,1:T(4,128)S(1)} %get-tuple-element.15), channel_id=1, source_target_pairs={{16,0},{0,16},{17,1},{1,17},{18,2},{2,18},{19,3},{3,19},{20,4},{4,... | collective-permute-start | bytes 55736 | tf_op jit(solution)/shard_map/ppermute | solution.py:35
  62.8 4.5 %collective-permute-start.2 = (f32[4,5,1,129]{3,0,2,1:T(4,128)S(1)}, f32[4,5,1,129]{3,0,2,1:T(4,128)S(1)}, u32[]{:S(2)}, u32[]{:S(2)}) collective-permute-start(f32[4,5,1,129]{3,0,2,1:T(4,128)S(1)} %get-tuple-element.12), channel_id=1, source_target_pairs={{0,4},{4,8},{8,12},{12,0},{1,5},{5,9},{9,13},{13,1},{2,6},{6,10},{... | collective-permute-start | bytes 30968 | tf_op jit(solution)/shard_map/ppermute | solution.py:33
  63.5 3.8 %collective-permute-start.3 = (f32[4,5,1,129]{3,0,2,1:T(4,128)S(1)}, f32[4,5,1,129]{3,0,2,1:T(4,128)S(1)}, u32[]{:S(2)}, u32[]{:S(2)}) collective-permute-start(f32[4,5,1,129]{3,0,2,1:T(4,128)S(1)} %get-tuple-element.13), channel_id=1, source_target_pairs={{4,0},{8,4},{12,8},{0,12},{5,1},{9,5},{13,9},{1,13},{6,2},{10,6},{... | collective-permute-start | bytes 30968 | tf_op jit(solution)/shard_map/ppermute | solution.py:35
  67.5 5.0 %collective-permute-start.4 = (f32[4,5,9,1]{3,0,2,1:T(4,128)S(1)}, f32[4,5,9,1]{3,0,2,1:T(4,128)S(1)}, u32[]{:S(2)}, u32[]{:S(2)}) collective-permute-start(f32[4,5,9,1]{3,0,2,1:T(4,128)S(1)} %get-tuple-element.10), channel_id=1, source_target_pairs={{0,1},{1,2},{2,3},{3,0},{4,5},{5,6},{6,7},{7,4},{8,9},{9,10},{10,1... | collective-permute-start | bytes 2168 | tf_op jit(solution)/shard_map/ppermute | solution.py:33
  71.0 4.0 %collective-permute-start.5 = (f32[4,5,9,1]{3,0,2,1:T(4,128)S(1)}, f32[4,5,9,1]{3,0,2,1:T(4,128)S(1)}, u32[]{:S(2)}, u32[]{:S(2)}) collective-permute-start(f32[4,5,9,1]{3,0,2,1:T(4,128)S(1)} %get-tuple-element.11), channel_id=1, source_target_pairs={{1,0},{2,1},{3,2},{0,3},{5,4},{6,5},{7,6},{4,7},{9,8},{10,9},{11,1... | collective-permute-start | bytes 2168 | tf_op jit(solution)/shard_map/ppermute | solution.py:35
